TPU v7x, 32 devices: a whole 2x2x4 slice. The times are simulated.
32 devices in a mesh: dp: 2 (over y), expert: 4 (over z), ffn: 4 (over x, core).
Axes of the slice: x: 2, y: 2, z: 4, core: 2. Of those that a mesh axis runs over, the one named last changes fastest.
Arguments:
- tokens: bfloat16 [512, 4096], P('expert'), may hold values from -6 to 6
- expert_ids: int32 [512, 2], P('expert'), may hold values from 0 to 3, all different within a row; in each aligned block of 128 rows (0 to 127, 128 to 255, ...) at most 64 rows name the same one
- route_weight: float32 [512, 2], P('expert'), may hold values from 0.05 to 1
- cotangent: bfloat16 [512, 4096], P('expert'), may hold values from -40 to 40
- w_gate: bfloat16 [4, 7168, 4096], P('expert', ('dp', 'ffn')), may hold values from -0.09375 to 0.09375
- w_up: bfloat16 [4, 7168, 4096], P('expert', ('dp', 'ffn')), may hold values from -0.09375 to 0.09375
- w_down: bfloat16 [4, 7168, 4096], P('expert', ('dp', 'ffn')), may hold values from -0.0625 to 0.0625
Outputs:
- layer_out: bfloat16 [512, 4096], P('expert', ('dp', 'ffn'))
- ascent_gate: bfloat16 [4, 7168, 4096], P('expert', ('dp', 'ffn'))
- ascent_up: bfloat16 [4, 7168, 4096], P('expert', ('dp', 'ffn'))
- ascent_down: bfloat16 [4, 7168, 4096], P('expert', ('dp', 'ffn'))
Inputs may be any that keep to these rules, and one draw needn't show every extreme that they name: `expert_ids`: each row names two different experts. Among the rows of one aligned block of 128 no expert is named more than 64 times; in every draw some block names some expert exactly 64 times.
All inputs are finite; a program needn't handle non-finite values.
Results may differ from a plain program's by a relative error of at most 0.017.
Values may be sent and summed in bfloat16 or wider, within the bound.
A program may use at most 128 MiB of HBM per device.

v0:
```python
import jax
import jax.numpy as jnp
from jax import lax
from jax.sharding import PartitionSpec as P

FF = 7168


def silu_parts(pre_act):
    sigmoid_value = jax.nn.sigmoid(pre_act)
    return (pre_act * sigmoid_value, sigmoid_value * (1.0 + pre_act * (1.0 - sigmoid_value)))


def against_rows(left_rows, right_rows):
    return lax.dot_general(
        left_rows, right_rows, (((0,), (0,)), ((), ())), preferred_element_type=jnp.float32
    )


def across_width(left_rows, weight):
    return lax.dot_general(
        left_rows, weight, (((1,), (1,)), ((), ())), preferred_element_type=jnp.float32
    )


def squares_of(matrix):
    return jnp.sum(matrix * matrix)


def on_device(tokens, expert_ids, route_weight, cotangent, w_gate, w_up, w_down):
    tok_rows, feature_width = tokens.shape
    experts = lax.axis_size("expert")
    groups = lax.axis_size(("dp", "ffn"))
    capacity = tok_rows // 2
    slot_count = experts * capacity
    column_width = feature_width // groups
    chosen = expert_ids[:, :, None] == jnp.arange(experts, dtype=jnp.int32)[None, None, :]
    per_token = jnp.sum(chosen.astype(jnp.int32), axis=1)
    earlier = jnp.cumsum(per_token, axis=0) - per_token
    position = jnp.sum(jnp.where(chosen, earlier[:, None, :], 0), axis=2)
    slot_index = expert_ids * capacity + position
    slot_hot = slot_index[:, :, None] == jnp.arange(slot_count, dtype=jnp.int32)[None, None, :]
    hot_all = slot_hot.reshape(tok_rows * 2, slot_count).astype(jnp.bfloat16)
    scaled = (route_weight[:, :, None] * cotangent.astype(jnp.float32)[:, None, :]).astype(
        jnp.bfloat16
    )
    token_slots = against_rows(hot_all, jnp.repeat(tokens, 2, axis=0)).astype(jnp.bfloat16)
    grad_slots = against_rows(hot_all, scaled.reshape(tok_rows * 2, feature_width)).astype(
        jnp.bfloat16
    )
    token_cube = token_slots.reshape(experts, capacity, feature_width)
    grad_cube = grad_slots.reshape(experts, capacity, feature_width)
    column_start = lax.axis_index(("dp", "ffn")) * column_width
    token_part = lax.dynamic_slice_in_dim(token_cube, column_start, column_width, 2)
    grad_part = lax.dynamic_slice_in_dim(grad_cube, column_start, column_width, 2)
    received = (
        lax.all_to_all(token_part, "expert", split_axis=0, concat_axis=0, tiled=True),
        lax.all_to_all(grad_part, "expert", split_axis=0, concat_axis=0, tiled=True),
    )
    slot_rows, slot_grads = (
        lax.all_gather(
            received[0].reshape(slot_count, column_width), ("dp", "ffn"), axis=1, tiled=True
        ),
        lax.all_gather(
            received[1].reshape(slot_count, column_width), ("dp", "ffn"), axis=1, tiled=True
        ),
    )
    gate_weight = w_gate[0]
    up_weight = w_up[0]
    down_weight = w_down[0]
    pre_gate = across_width(slot_rows, gate_weight)
    pre_up = across_width(slot_rows, up_weight)
    activated, derivative = silu_parts(pre_gate)
    hidden = (activated * pre_up).astype(jnp.bfloat16)
    partial_value = jnp.dot(hidden, down_weight, preferred_element_type=jnp.float32)
    grad_down = against_rows(hidden, slot_grads)
    grad_hidden = across_width(slot_grads, down_weight)
    delta_gate = (grad_hidden * pre_up * derivative).astype(jnp.bfloat16)
    delta_up = (grad_hidden * activated).astype(jnp.bfloat16)
    grad_gate = against_rows(delta_gate, slot_rows)
    grad_up = against_rows(delta_up, slot_rows)
    sum_squares = lax.psum(
        squares_of(grad_gate) + squares_of(grad_up) + squares_of(grad_down), ("dp", "expert", "ffn")
    )
    summed = lax.psum_scatter(
        partial_value.astype(jnp.bfloat16), ("dp", "ffn"), scatter_dimension=1, tiled=True
    )
    summed = summed.reshape(experts, capacity, column_width)
    returned_rows = lax.all_to_all(
        summed, "expert", split_axis=0, concat_axis=0, tiled=True
    ).reshape(slot_count, column_width)
    picked = jnp.dot(hot_all, returned_rows, preferred_element_type=jnp.float32).reshape(
        tok_rows, 2, column_width
    )
    layer_out = jnp.sum(route_weight[:, :, None] * picked, axis=1).astype(jnp.bfloat16)
    inv_rms = lax.rsqrt(sum_squares / (3.0 * experts * FF * feature_width) + 1e-06)
    return (
        layer_out,
        (grad_gate * inv_rms).astype(jnp.bfloat16)[None],
        (grad_up * inv_rms).astype(jnp.bfloat16)[None],
        (grad_down * inv_rms).astype(jnp.bfloat16)[None],
    )


def solution(mesh):
    return jax.shard_map(
        on_device,
        mesh=mesh,
        in_specs=(
            P("expert", None),
            P("expert", None),
            P("expert", None),
            P("expert", None),
            P("expert", ("dp", "ffn"), None),
            P("expert", ("dp", "ffn"), None),
            P("expert", ("dp", "ffn"), None),
        ),
        out_specs=(
            P("expert", ("dp", "ffn")),
            P("expert", ("dp", "ffn"), None),
            P("expert", ("dp", "ffn"), None),
            P("expert", ("dp", "ffn"), None),
        ),
        check_vma=False,
    )
```

profile of v0, /device:TPU:0, one launch (start us, length us, event | category | flops | bytes accessed | tf_op | source)
XLA Modules:
  0.0 195.2 jit_solution(6774078264472581371)
XLA Ops:
  7.2 0.0 copy-start
  7.2 0.0 copy-start.4
  7.2 0.0 copy-start.6
  7.2 0.0 all-gather.3.cloned.1.call-start
  7.3 0.8 convert_reduce_fusion
  8.1 0.1 copy.12
  8.2 0.2 reduce_window_sum.11
  8.4 0.1 copy.14
  8.4 0.7 select_reduce_fusion
  9.2 0.7 multiply_add_fusion
  9.8 0.0 copy-done
  9.8 0.7 fusion.14
  10.6 15.1 %all_to_all.15 = bf16[4,64,512]{2,1,0:T(8,128)(2,1)} all-to-all(bf16[4,64,512]{2,1,0:T(8,128)(2,1)S(1)} %constant_dynamic-slice_fusion), channel_id=1, replica_groups=mesh['dp'=2,'expert'=4,'ffn'=4] {'expert'}, dimensions={0} | all-to-all | bytes 524288 | tf_op jit(solution)/shard_map/all_to_all | solution.py:57
  25.7 0.0 all-gather.3.cloned.1.call-update
  25.8 0.0 all-gather.5.cloned.1.call-start
  25.8 0.0 copy-done.4
  25.8 0.2 convert_element_type.45
  26.0 0.0 copy-done.6
  26.0 0.8 fusion.15
  26.9 11.1 %all_to_all.16 = bf16[4,64,512]{2,1,0:T(8,128)(2,1)} all-to-all(bf16[4,64,512]{2,1,0:T(8,128)(2,1)S(1)} %constant_dynamic-slice_fusion.1), channel_id=1, replica_groups=mesh['dp'=2,'expert'=4,'ffn'=4] {'expert'}, dimensions={0} | all-to-all | bytes 524288 | tf_op jit(solution)/shard_map/all_to_all | solution.py:58
  38.0 0.0 all-gather.5.cloned.1.call-update
  38.0 0.2 reduce-scatter.2.cloned.1.call-start
  38.3 14.9 %all-gather.3.cloned.1.call-done = bf16[256,4096]{1,0:T(8,128)(2,1)} async-done(((bf16[256,512]{1,0:T(8,128)(2,1)}), bf16[256,4096]{1,0:T(8,128)(2,1)}) %all-gather.3.cloned.1.call-update) | async-done | bytes 2097168 | tf_op jit(solution)/shard_map/all_gather | solution.py:61
  53.1 0.0 copy-start.2
  53.1 0.0 slice-start
  53.1 6.2 %fusion.9 = f32[256,896]{1,0:T(8,128)S(1)} fusion(bf16[256,4096]{1,0:T(8,128)(2,1)} %all-gather.3.cloned.1.call-done, bf16[1,896,4096]{2,1,0:T(8,128)(2,1)} %param.11), kind=kOutput, calls=%fused_computation.15 | convolution fusion | flops 1879048192 | bytes 10354688 | tf_op jit(solution)/shard_map/dot_general | solution.py:21
  59.3 0.0 copy-done.2
  59.4 0.0 slice-start.1
  59.4 6.7 %multiply_convert_fusion.7 = (bf16[256,896]{1,0:T(8,128)(2,1)S(1)}, f32[256,896]{1,0:T(8,128)}) fusion(f32[256,896]{1,0:T(8,128)S(1)} %fusion.9, bf16[256,4096]{1,0:T(8,128)(2,1)S(1)} %copy-done.2, bf16[1,896,4096]{2,1,0:T(8,128)(2,1)} %param.12), kind=kOutput, calls=%fused_computation.30 | convolution fusion | flops 1880424448 | bytes 11730944 | tf_op jit(solution)/shard_map/dot_general | solution.py:21
  66.1 0.0 copy-start.5
  66.1 0.8 copy-done.5
  66.9 0.0 slice-done
  66.9 0.0 slice-done.1
  66.9 3.7 %fusion.11 = bf16[256,4096]{1,0:T(8,128)(2,1)} fusion(bf16[256,896]{1,0:T(8,128)(2,1)S(1)} %get-tuple-element.4, bf16[1,896,4096]{2,1,0:T(8,128)(2,1)S(1)} %bitcast.56), kind=kOutput, calls=%fused_computation.19 | convolution fusion | flops 1880096768 | bytes 9895936 | tf_op jit(solution)/shard_map/dot_general | solution.py:75
  70.5 0.0 reduce-scatter.2.cloned.1.call-update
  70.5 12.6 %all-gather.5.cloned.1.call-done = bf16[256,4096]{1,0:T(8,128)(2,1)} async-done(((bf16[256,512]{1,0:T(8,128)(2,1)}), bf16[256,4096]{1,0:T(8,128)(2,1)}) %all-gather.5.cloned.1.call-update) | async-done | bytes 2097168 | tf_op jit(solution)/shard_map/all_gather | solution.py:64
  83.1 6.1 %fusion.3 = f32[256,896]{1,0:T(8,128)S(1)} fusion(bf16[256,4096]{1,0:T(8,128)(2,1)} %all-gather.5.cloned.1.call-done, bf16[1,896,4096]{2,1,0:T(8,128)(2,1)} %param.13), kind=kOutput, calls=%fused_computation.9 | convolution fusion | flops 1879048192 | bytes 10354688 | tf_op jit(solution)/shard_map/dot_general | solution.py:21
  89.3 0.0 copy-done.3
  89.3 8.6 %multiply_reduce_fusion.2 = (f32[]{:T(128)}, f32[896,4096]{1,0:T(8,128)}) fusion(bf16[256,4096]{1,0:T(8,128)(2,1)S(1)} %copy-done.2, f32[256,896]{1,0:T(8,128)S(1)} %fusion.9, f32[256,896]{1,0:T(8,128)S(1)} %fusion.3, f32[256,896]{1,0:T(8,128)S(1)} %copy-done.3), kind=kOutput, calls=%fused_computation.5 | convolution fusion | flops 1888681984 | bytes 19529732 | tf_op jit(solution)/shard_map/dot_general | solution.py:15
  97.9 8.3 %multiply_reduce_fusion.1 = (f32[]{:T(128)}, f32[896,4096]{1,0:T(8,128)}) fusion(bf16[256,4096]{1,0:T(8,128)(2,1)S(1)} %copy-done.2, f32[256,896]{1,0:T(8,128)S(1)} %fusion.3, f32[256,896]{1,0:T(8,128)S(1)} %fusion.9), kind=kOutput, calls=%fused_computation.4 | convolution fusion | flops 1887764480 | bytes 18612228 | tf_op jit(solution)/shard_map/dot_general | solution.py:15
  107.5 9.8 %multiply_reduce_fusion = (f32[]{:T(128)}, f32[896,4096]{1,0:T(8,128)}) fusion(bf16[256,896]{1,0:T(8,128)(2,1)} %copy-done.5, bf16[256,4096]{1,0:T(8,128)(2,1)} %all-gather.5.cloned.1.call-done), kind=kOutput, calls=%fused_computation.3 | convolution fusion | flops 1886388224 | bytes 17235972 | tf_op jit(solution)/shard_map/dot_general | solution.py:15
  118.0 39.8 %psum.7 = f32[]{:T(128)} all-reduce(f32[]{:T(128)S(6)} %add.35), channel_id=1, replica_groups=mesh['dp'=2,'expert'=4,'ffn'=4] {'dp','expert','ffn'}, use_global_device_ids=true, to_apply=%region_8.9 | all-reduce | flops 1 | bytes 8 | tf_op jit(solution)/shard_map/psum | solution.py:82
  158.4 15.5 %fusion = (bf16[1,896,4096]{2,1,0:T(8,128)(2,1)}, bf16[1,896,4096]{2,1,0:T(8,128)(2,1)}) fusion(f32[896,4096]{1,0:T(8,128)} %get-tuple-element.7, f32[]{:T(128)S(6)} %rsqrt.3, f32[896,4096]{1,0:T(8,128)} %get-tuple-element.9), kind=kLoop, calls=%fused_computation.6 | loop fusion | flops 14680064 | bytes 44040196 | tf_op jit(solution)/shard_map/broadcast_in_dim | solution.py:99
  173.9 3.6 %all-to-all-start.1 = ((bf16[4,64,512]{2,1,0:T(8,128)(2,1)}), bf16[4,64,512]{2,1,0:T(8,128)(2,1)S(1)}, u32[]{:S(2)}, u32[]{:S(2)}) async-start(bf16[4,64,512]{2,1,0:T(8,128)(2,1)} %bitcast.53), calls=%async_computation.2 | async-start | bytes 524288 | tf_op jit(solution)/shard_map/all_to_all | solution.py:89
  177.5 10.3 %fusion.2 = bf16[1,896,4096]{2,1,0:T(8,128)(2,1)} fusion(f32[896,4096]{1,0:T(8,128)} %get-tuple-element.11, f32[]{:T(128)S(6)} %rsqrt.3), kind=kLoop, calls=%fused_computation.8 | loop fusion | flops 7340032 | bytes 22020100 | tf_op jit(solution)/shard_map/broadcast_in_dim | solution.py:101
  187.7 0.0 all-to-all-done.1
  187.7 0.9 fusion.18
  188.7 0.0 copy-done.1
  (7 shorter events, 0.1 us)
Async XLA Ops:
  7.2 2.7 %copy-start = (bf16[128,4096]{1,0:T(8,128)(2,1)S(1)}, bf16[128,4096]{1,0:T(8,128)(2,1)}, u32[]{:S(2)}) copy-start(bf16[128,4096]{1,0:T(8,128)(2,1)} %param.7) | copy-start | bytes 3145732
  7.2 18.6 %copy-start.4 = (bf16[128,4096]{1,0:T(8,128)(2,1)S(1)}, bf16[128,4096]{1,0:T(8,128)(2,1)}, u32[]{:S(2)}) copy-start(bf16[128,4096]{1,0:T(8,128)(2,1)} %param.10) | copy-start | bytes 3145732
  7.2 18.8 %copy-start.6 = (f32[128,2]{0,1:T(2,128)S(1)}, f32[128,2]{0,1:T(2,128)}, u32[]{:S(2)}) copy-start(f32[128,2]{0,1:T(2,128)} %param.9) | copy-start | bytes 3076
  7.2 45.9 %all-gather.3.cloned.1.call-start = ((), (), s32[]{:S(2)}) async-start(), calls=%async_computation.4 | async-start | bytes 2359296 | tf_op jit(solution)/shard_map/all_gather | solution.py:61
  25.8 57.4 %all-gather.5.cloned.1.call-start = ((), (), s32[]{:S(2)}) async-start(), calls=%async_computation.6 | async-start | bytes 2359296 | tf_op jit(solution)/shard_map/all_gather | solution.py:64
  38.0 135.9 %reduce-scatter.2.cloned.1.call-start = ((), (), s32[]{:S(2)}) async-start(), calls=%async_computation.5 | async-start | bytes 2359296 | tf_op jit(solution)/shard_map/reduce_scatter | solution.py:85
  53.1 6.2 %copy-start.2 = (bf16[256,4096]{1,0:T(8,128)(2,1)S(1)}, bf16[256,4096]{1,0:T(8,128)(2,1)}, u32[]{:S(2)}) copy-start(bf16[256,4096]{1,0:T(8,128)(2,1)} %all-gather.3.cloned.1.call-done) | copy-start | bytes 6291460
  53.1 13.7 %slice-start = ((s8[7340032]{0:T(1024)(128)(4,1)}), s8[4194304]{0:T(1024)(128)(4,1)S(1)}, s32[]{:S(2)}) async-start(s8[7340032]{0:T(1024)(128)(4,1)} %bitcast.55), calls=%async_computation.7 | async-start | bytes 8388608
  59.4 7.5 %slice-start.1 = ((s8[7340032]{0:T(1024)(128)(4,1)}), s8[3145728]{0:T(1024)(128)(4,1)S(1)}, s32[]{:S(2)}) async-start(s8[7340032]{0:T(1024)(128)(4,1)} %bitcast.55), calls=%async_computation.8 | async-start | bytes 6291456
  66.1 0.8 copy-start.5
  83.1 6.2 %copy-start.3 = (f32[256,896]{1,0:T(8,128)S(1)}, f32[256,896]{1,0:T(8,128)}, u32[]{:S(2)}) copy-start(f32[256,896]{1,0:T(8,128)} %get-tuple-element.5) | copy-start | bytes 2752516
  173.9 13.8 %all-to-all-start.1 = ((bf16[4,64,512]{2,1,0:T(8,128)(2,1)}), bf16[4,64,512]{2,1,0:T(8,128)(2,1)S(1)}, u32[]{:S(2)}, u32[]{:S(2)}) async-start(bf16[4,64,512]{2,1,0:T(8,128)(2,1)} %bitcast.53), calls=%async_computation.2 | async-start | bytes 524288 | tf_op jit(solution)/shard_map/all_to_all | solution.py:89
  177.5 11.2 %copy-start.1 = (bf16[128,4096]{1,0:T(8,128)(2,1)S(1)}, bf16[128,4096]{1,0:T(8,128)(2,1)}, u32[]{:S(2)}) copy-start(bf16[128,4096]{1,0:T(8,128)(2,1)} %param.7) | copy-start | bytes 3145732
Sparse Core Ops, SparseCore 0:
  25.9 27.1 all-gather.2
  55.0 28.0 all-gather.4
  87.0 41.6 reduce-scatter.1
where the time goes:
time: 196 us; the launch traced here: 195 us
  blocking collectives  66 us (34%)
  matrix products  51.9 us (26%)
  other arithmetic  28.4 us (14%)
  waiting for transfers between devices  27.5 us (14%)
  between operations  16.5 us (8%)
  starting transfers between devices  3.85 us (2%)
    psum x1, blocking collectives, on_device(): lax.psum(squares_of(grad_gate) + squares_of(grad_up) + squares_of(grad_do...  39.8 us
    dot_general x5, matrix products, against_rows(): lax.dot_general(left_rows, right_rows, (((0,), (0,)), ((), ())), preferre...  28.3 us
    dot_general x3, matrix products, across_width(): lax.dot_general(left_rows, weight, (((1,), (1,)), ((), ())), preferred_el...  19.1 us
    broadcast_in_dim x1, other arithmetic, on_device(): (grad_gate * inv_rms).astype(jnp.bfloat16)[None]  15.5 us
    all_to_all x1, blocking collectives, on_device(): lax.all_to_all(token_part, 'expert', split_axis=0, concat_axis=0, tiled=T...  15.1 us
    all_gather x1, waiting for transfers between devices, on_device(): lax.all_gather(received[0].reshape(slot_count, column_width), ('dp', 'ffn...  14.9 us
    all_gather x1, waiting for transfers between devices, on_device(): lax.all_gather(received[1].reshape(slot_count, column_width), ('dp', 'ffn...  12.6 us
    all_to_all x1, blocking collectives, on_device(): lax.all_to_all(grad_part, 'expert', split_axis=0, concat_axis=0, tiled=True)  11.1 us
  transfers between devices with their start and end apart: 4, of which 2 were waited for; matrix products, arithmetic and copies ran while one was open for 39% of the time, Pallas kernels for 0%

commit v1 on v0

--- a/solution.py
+++ b/solution.py
@@ -4,6 +4,11 @@
 from jax.sharding import PartitionSpec as P
 
 FF = 7168
+
+
+def stack_and_merge(shard, axis, along):
+    parts = lax.all_gather(shard, axis)
+    return jnp.concatenate(parts, axis=along)
 
 
 def silu_parts(pre_act):
@@ -61,9 +66,7 @@
         lax.all_gather(
             received[0].reshape(slot_count, column_width), ("dp", "ffn"), axis=1, tiled=True
         ),
-        lax.all_gather(
-            received[1].reshape(slot_count, column_width), ("dp", "ffn"), axis=1, tiled=True
-        ),
+        stack_and_merge(received[1].reshape(slot_count, column_width), ("dp", "ffn"), 1),
     )
     gate_weight = w_gate[0]
     up_weight = w_up[0]

time: 196 us -> 199 us (1.015)
  local copies, waits for them, and re-layouts: 1.04 us -> 4.07 us
    all_gather x0 -> x1, local copies, waits for them, and re-layouts: none -> 3.03 us  [stack_and_merge(): parts = lax.all_gather(shard, axis)]
  transfers between devices with their start and end apart: 4 -> 4, of which waited for: 2 -> 2; matrix products, arithmetic and copies ran while one was open for 39% -> 40% of each run, Pallas kernels for 0% -> 0%
where the time goes in v1:
time: 199 us; the launch traced here: 198 us
  blocking collectives  65.6 us (33%)
  matrix products  52.6 us (26%)
  other arithmetic  28.4 us (14%)
  waiting for transfers between devices  27.1 us (14%)
  between operations  16.6 us (8%)
  local copies, waits for them, and re-layouts  4.07 us (2%)
  starting transfers between devices  3.67 us (2%)
    psum x1, blocking collectives, on_device(): lax.psum(squares_of(grad_gate) + squares_of(grad_up) + squares_of(grad_do...  39.4 us
    dot_general x5, matrix products, against_rows(): lax.dot_general(left_rows, right_rows, (((0,), (0,)), ((), ())), preferre...  29.2 us
    dot_general x3, matrix products, across_width(): lax.dot_general(left_rows, weight, (((1,), (1,)), ((), ())), preferred_el...  18.8 us
    broadcast_in_dim x1, other arithmetic, on_device(): (grad_gate * inv_rms).astype(jnp.bfloat16)[None]  15.5 us
    all_to_all x1, blocking collectives, on_device(): lax.all_to_all(token_part, 'expert', split_axis=0, concat_axis=0, tiled=T...  15.1 us
    all_gather x1, waiting for transfers between devices, on_device(): lax.all_gather(received[0].reshape(slot_count, column_width), ('dp', 'ffn...  15 us
    all_gather x1, waiting for transfers between devices, stack_and_merge(): parts = lax.all_gather(shard, axis)  12 us
    all_to_all x1, blocking collectives, on_device(): lax.all_to_all(grad_part, 'expert', split_axis=0, concat_axis=0, tiled=True)  11.1 us
  transfers between devices with their start and end apart: 4, of which 2 were waited for; matrix products, arithmetic and copies ran while one was open for 40% of the time, Pallas kernels for 0%

profile of v1, /device:TPU:0, one launch (start us, length us, event | category | flops | bytes accessed | tf_op | source)
XLA Modules:
  0.0 198.0 jit_solution(4676071659224278645)
XLA Ops:
  7.2 0.0 copy-start
  7.2 0.0 copy-start.5
  7.2 0.0 copy-start.7
  7.2 0.0 all-gather.3.cloned.1.call-start
  7.3 0.8 convert_reduce_fusion
  8.1 0.1 copy.18
  8.2 0.2 reduce_window_sum.11
  8.4 0.1 copy.20
  8.4 0.7 select_reduce_fusion
  9.2 0.7 multiply_add_fusion
  9.8 0.0 copy-done
  9.8 0.7 fusion.14
  10.6 15.1 %all_to_all.15 = bf16[4,64,512]{2,1,0:T(8,128)(2,1)} all-to-all(bf16[4,64,512]{2,1,0:T(8,128)(2,1)S(1)} %constant_dynamic-slice_fusion), channel_id=1, replica_groups=mesh['dp'=2,'expert'=4,'ffn'=4] {'expert'}, dimensions={0} | all-to-all | bytes 524288 | tf_op jit(solution)/shard_map/all_to_all | solution.py:62
  25.7 0.0 all-gather.3.cloned.1.call-update
  25.8 0.0 all-gather.5.cloned.1.call-start
  25.8 0.0 copy-done.5
  25.8 0.2 convert_element_type.45
  26.0 0.0 copy-done.7
  26.0 0.8 fusion.15
  26.9 11.1 %all_to_all.16 = bf16[4,64,512]{2,1,0:T(8,128)(2,1)} all-to-all(bf16[4,64,512]{2,1,0:T(8,128)(2,1)S(1)} %constant_dynamic-slice_fusion.1), channel_id=1, replica_groups=mesh['dp'=2,'expert'=4,'ffn'=4] {'expert'}, dimensions={0} | all-to-all | bytes 524288 | tf_op jit(solution)/shard_map/all_to_all | solution.py:63
  38.0 0.0 all-gather.5.cloned.1.call-update
  38.0 0.0 reduce-scatter.2.cloned.1.call-start
  38.1 15.0 %all-gather.3.cloned.1.call-done = bf16[256,4096]{1,0:T(8,128)(2,1)} async-done(((bf16[256,512]{1,0:T(8,128)(2,1)}), bf16[256,4096]{1,0:T(8,128)(2,1)}) %all-gather.3.cloned.1.call-update) | async-done | bytes 2097168 | tf_op jit(solution)/shard_map/all_gather | solution.py:66
  53.1 6.2 %fusion.9 = f32[256,896]{1,0:T(8,128)S(1)} fusion(bf16[256,4096]{1,0:T(8,128)(2,1)} %all-gather.3.cloned.1.call-done, bf16[1,896,4096]{2,1,0:T(8,128)(2,1)} %param.11), kind=kOutput, calls=%fused_computation.15 | convolution fusion | flops 1879048192 | bytes 10354688 | tf_op jit(solution)/shard_map/dot_general | solution.py:26
  59.3 0.0 copy-done.2
  59.4 0.0 slice-start.1
  59.4 7.0 %multiply_convert_fusion.7 = (bf16[256,896]{1,0:T(8,128)(2,1)S(1)}, f32[256,896]{1,0:T(8,128)}) fusion(f32[256,896]{1,0:T(8,128)S(1)} %fusion.9, bf16[256,4096]{1,0:T(8,128)(2,1)S(1)} %copy-done.2, bf16[1,896,4096]{2,1,0:T(8,128)(2,1)} %param.12), kind=kOutput, calls=%fused_computation.30 | convolution fusion | flops 1880424448 | bytes 11730944 | tf_op jit(solution)/shard_map/dot_general | solution.py:26
  66.3 0.8 copy-done.6
  67.1 0.0 slice-done
  67.1 0.0 slice-done.1
  67.1 3.7 %fusion.11 = bf16[256,4096]{1,0:T(8,128)(2,1)} fusion(bf16[256,896]{1,0:T(8,128)(2,1)S(1)} %get-tuple-element.4, bf16[1,896,4096]{2,1,0:T(8,128)(2,1)S(1)} %bitcast.61), kind=kOutput, calls=%fused_computation.19 | convolution fusion | flops 1880096768 | bytes 9895936 | tf_op jit(solution)/shard_map/dot_general | solution.py:78
  70.8 0.0 reduce-scatter.2.cloned.1.call-update
  70.8 12.0 %all-gather.5.cloned.1.call-done = bf16[8,256,512]{2,1,0:T(8,128)(2,1)} async-done(((bf16[1,256,512]{2,1,0:T(8,128)(2,1)}), bf16[8,256,512]{2,1,0:T(8,128)(2,1)}) %all-gather.5.cloned.1.call-update) | async-done | bytes 2097168 | tf_op jit(solution)/shard_map/all_gather | solution.py:10
  82.8 3.0 %copy.21 = bf16[8,256,512]{1,2,0:T(8,128)(2,1)S(1)} copy(bf16[8,256,512]{2,1,0:T(8,128)(2,1)} %all-gather.5.cloned.1.call-done) | data formatting | bytes 4194304 | tf_op jit(solution)/shard_map/all_gather | solution.py:10
  85.8 0.0 copy-start.3
  85.9 0.0 copy-start.4
  85.9 5.6 %fusion.3 = f32[256,896]{1,0:T(8,128)S(1)} fusion(bf16[256,4096]{0,1:T(8,128)(2,1)S(1)} %bitcast.52, bf16[1,896,4096]{2,1,0:T(8,128)(2,1)} %param.13), kind=kOutput, calls=%fused_computation.9 | convolution fusion | flops 1879048192 | bytes 10354688 | tf_op jit(solution)/shard_map/dot_general | solution.py:26
  91.5 0.0 copy-done.3
  91.5 0.0 copy-done.4
  91.5 8.6 %multiply_reduce_fusion.2 = (f32[]{:T(128)}, f32[896,4096]{1,0:T(8,128)}) fusion(bf16[256,4096]{1,0:T(8,128)(2,1)S(1)} %copy-done.3, f32[256,896]{1,0:T(8,128)S(1)} %fusion.9, f32[256,896]{1,0:T(8,128)S(1)} %fusion.3, f32[256,896]{1,0:T(8,128)S(1)} %copy-done.4), kind=kOutput, calls=%fused_computation.5 | convolution fusion | flops 1888681984 | bytes 19529732 | tf_op jit(solution)/shard_map/dot_general | solution.py:20
  100.1 8.0 %multiply_reduce_fusion.1 = (f32[]{:T(128)}, f32[896,4096]{1,0:T(8,128)}) fusion(bf16[256,4096]{1,0:T(8,128)(2,1)S(1)} %copy-done.3, f32[256,896]{1,0:T(8,128)S(1)} %fusion.3, f32[256,896]{1,0:T(8,128)S(1)} %fusion.9), kind=kOutput, calls=%fused_computation.4 | convolution fusion | flops 1887764480 | bytes 18612228 | tf_op jit(solution)/shard_map/dot_general | solution.py:20
  109.5 11.0 %multiply_reduce_fusion = (f32[]{:T(128)}, f32[896,4096]{1,0:T(8,128)}) fusion(bf16[256,896]{1,0:T(8,128)(2,1)} %copy-done.6, bf16[256,4096]{0,1:T(8,128)(2,1)S(1)} %bitcast.53), kind=kOutput, calls=%fused_computation.3 | convolution fusion | flops 1886388224 | bytes 17235972 | tf_op jit(solution)/shard_map/dot_general | solution.py:20
  121.1 39.4 %psum.7 = f32[]{:T(128)} all-reduce(f32[]{:T(128)S(6)} %add.35), channel_id=1, replica_groups=mesh['dp'=2,'expert'=4,'ffn'=4] {'dp','expert','ffn'}, use_global_device_ids=true, to_apply=%region_8.9 | all-reduce | flops 1 | bytes 8 | tf_op jit(solution)/shard_map/psum | solution.py:85
  161.2 15.5 %fusion = (bf16[1,896,4096]{2,1,0:T(8,128)(2,1)}, bf16[1,896,4096]{2,1,0:T(8,128)(2,1)}) fusion(f32[896,4096]{1,0:T(8,128)} %get-tuple-element.7, f32[]{:T(128)S(6)} %rsqrt.3, f32[896,4096]{1,0:T(8,128)} %get-tuple-element.9), kind=kLoop, calls=%fused_computation.6 | loop fusion | flops 14680064 | bytes 44040196 | tf_op jit(solution)/shard_map/broadcast_in_dim | solution.py:102
  176.7 3.5 %all-to-all-start.1 = ((bf16[4,64,512]{2,1,0:T(8,128)(2,1)}), bf16[4,64,512]{2,1,0:T(8,128)(2,1)S(1)}, u32[]{:S(2)}, u32[]{:S(2)}) async-start(bf16[4,64,512]{2,1,0:T(8,128)(2,1)} %bitcast.58), calls=%async_computation.2 | async-start | bytes 524288 | tf_op jit(solution)/shard_map/all_to_all | solution.py:92
  180.3 10.3 %fusion.2 = bf16[1,896,4096]{2,1,0:T(8,128)(2,1)} fusion(f32[896,4096]{1,0:T(8,128)} %get-tuple-element.11, f32[]{:T(128)S(6)} %rsqrt.3), kind=kLoop, calls=%fused_computation.8 | loop fusion | flops 7340032 | bytes 22020100 | tf_op jit(solution)/shard_map/broadcast_in_dim | solution.py:104
  190.5 0.0 all-to-all-done.1
  190.5 0.9 fusion.18
  (10 shorter events, 0.1 us)
Async XLA Ops:
  7.2 2.7 %copy-start = (bf16[128,4096]{1,0:T(8,128)(2,1)S(1)}, bf16[128,4096]{1,0:T(8,128)(2,1)}, u32[]{:S(2)}) copy-start(bf16[128,4096]{1,0:T(8,128)(2,1)} %param.7) | copy-start | bytes 3145732
  7.2 18.6 %copy-start.5 = (bf16[128,4096]{1,0:T(8,128)(2,1)S(1)}, bf16[128,4096]{1,0:T(8,128)(2,1)}, u32[]{:S(2)}) copy-start(bf16[128,4096]{1,0:T(8,128)(2,1)} %param.10) | copy-start | bytes 3145732
  7.2 18.8 %copy-start.7 = (f32[128,2]{0,1:T(2,128)S(1)}, f32[128,2]{0,1:T(2,128)}, u32[]{:S(2)}) copy-start(f32[128,2]{0,1:T(2,128)} %param.9) | copy-start | bytes 3076
  7.2 45.9 %all-gather.3.cloned.1.call-start = ((), (), s32[]{:S(2)}) async-start(), calls=%async_computation.4 | async-start | bytes 2359296 | tf_op jit(solution)/shard_map/all_gather | solution.py:66
  25.8 57.1 %all-gather.5.cloned.1.call-start = ((), (), s32[]{:S(2)}) async-start(), calls=%async_computation.6 | async-start | bytes 2359296 | tf_op jit(solution)/shard_map/all_gather | solution.py:10
  38.0 138.7 %reduce-scatter.2.cloned.1.call-start = ((), (), s32[]{:S(2)}) async-start(), calls=%async_computation.5 | async-start | bytes 2359296 | tf_op jit(solution)/shard_map/reduce_scatter | solution.py:88
  53.1 6.2 %copy-start.2 = (bf16[256,4096]{1,0:T(8,128)(2,1)S(1)}, bf16[256,4096]{1,0:T(8,128)(2,1)}, u32[]{:S(2)}) copy-start(bf16[256,4096]{1,0:T(8,128)(2,1)} %all-gather.3.cloned.1.call-done) | copy-start | bytes 6291460
  53.1 14.0 %slice-start = ((s8[7340032]{0:T(1024)(128)(4,1)}), s8[4194304]{0:T(1024)(128)(4,1)S(1)}, s32[]{:S(2)}) async-start(s8[7340032]{0:T(1024)(128)(4,1)} %bitcast.60), calls=%async_computation.7 | async-start | bytes 8388608
  59.4 7.7 %slice-start.1 = ((s8[7340032]{0:T(1024)(128)(4,1)}), s8[3145728]{0:T(1024)(128)(4,1)S(1)}, s32[]{:S(2)}) async-start(s8[7340032]{0:T(1024)(128)(4,1)} %bitcast.60), calls=%async_computation.8 | async-start | bytes 6291456
  66.3 0.8 copy-start.6
  85.8 5.6 %copy-start.3 = (bf16[256,4096]{1,0:T(8,128)(2,1)S(1)}, bf16[256,4096]{1,0:T(8,128)(2,1)}, u32[]{:S(2)}) copy-start(bf16[256,4096]{1,0:T(8,128)(2,1)} %all-gather.3.cloned.1.call-done) | copy-start | bytes 6291460
  85.9 5.6 %copy-start.4 = (f32[256,896]{1,0:T(8,128)S(1)}, f32[256,896]{1,0:T(8,128)}, u32[]{:S(2)}) copy-start(f32[256,896]{1,0:T(8,128)} %get-tuple-element.5) | copy-start | bytes 2752516
  176.7 13.8 %all-to-all-start.1 = ((bf16[4,64,512]{2,1,0:T(8,128)(2,1)}), bf16[4,64,512]{2,1,0:T(8,128)(2,1)S(1)}, u32[]{:S(2)}, u32[]{:S(2)}) async-start(bf16[4,64,512]{2,1,0:T(8,128)(2,1)} %bitcast.58), calls=%async_computation.2 | async-start | bytes 524288 | tf_op jit(solution)/shard_map/all_to_all | solution.py:92
  180.3 11.2 %copy-start.1 = (bf16[128,4096]{1,0:T(8,128)(2,1)S(1)}, bf16[128,4096]{1,0:T(8,128)(2,1)}, u32[]{:S(2)}) copy-start(bf16[128,4096]{1,0:T(8,128)(2,1)} %param.7) | copy-start | bytes 3145732
Sparse Core Ops, SparseCore 0:
  25.9 27.1 all-gather.2
  55.0 27.7 all-gather.4
  86.7 41.1 reduce-scatter.1
